TPU v7x, 32 devices: a whole 2x2x4 slice. The times are simulated.
32 devices in a mesh: replica: 16 (over z, x, core), spatial: 2 (over y).
Axes of the slice: x: 2, y: 2, z: 4, core: 2. Of those that a mesh axis runs over, the one named last changes fastest.
Arguments:
- grads: bfloat16 [16, 2, 852992], P('replica', 'spatial'), may hold values from -6 to 6
- master: float32 [852992], P(('replica', 'spatial')), may hold values from -0.06 to 0.06
- velocity: float32 [852992], P(('replica', 'spatial')), may hold values from -0.3 to 0.3
- layer_offsets: int32 [6], replicated, may hold values from 0 to 852736, as said below
- layer_sizes: int32 [6], replicated, may hold values from 256 to 589824
- lars_skip: int32 [6], replicated, may hold values from 0 to 1
Outputs:
- new_weights: bfloat16 [852992], replicated
- new_master: float32 [852992], P(('replica', 'spatial'))
- new_velocity: float32 [852992], P(('replica', 'spatial'))
Inputs may be any that keep to these rules, and one draw needn't show every extreme that they name: layer_offsets, layer_sizes and lars_skip describe the six tensors (a 256 x 1024 convolution, a 256 x 256 x 9 convolution, and two gains and two shifts of 256 entries) laid end to end in some order without gaps, the last of them always a gain or a shift; lars_skip is 1 exactly for the gains and shifts.
All inputs are finite; a program needn't handle non-finite values.
Results may differ from a plain program's by a relative error of at most 0.001.
Values may be sent and summed in bfloat16 or wider, within the bound.
A program may use at most 64 MiB of HBM per device.

v0:
```python
import jax
import jax.numpy as jnp
from jax import lax
from jax.sharding import PartitionSpec as P


def shards(grads, master, velocity, layer_offsets, layer_sizes, lars_skip):
    n_rep = lax.axis_size("replica")
    n_spa = lax.axis_size("spatial")
    shard = master.shape[0]
    position = lax.axis_index(("replica", "spatial")) * shard + jnp.arange(shard, dtype=jnp.int32)
    inside = (position[None, :] >= layer_offsets[:, None]) & (
        position[None, :] < (layer_offsets + layer_sizes)[:, None]
    )
    onehot = inside.astype(jnp.float32)
    received = lax.all_to_all(
        grads[0, 0].reshape(n_rep, n_spa * shard),
        "replica",
        split_axis=0,
        concat_axis=0,
        tiled=True,
    )
    first = jnp.sum(received.astype(jnp.float32), axis=0)
    summed = lax.psum_scatter(
        first.reshape(n_spa, shard), "spatial", scatter_dimension=0, tiled=True
    )
    grad = summed.reshape(shard) / (n_rep * n_spa)
    gsq_local = jnp.dot(onehot, grad * grad, precision=lax.Precision.HIGHEST)
    wsq_local = jnp.dot(onehot, master * master, precision=lax.Precision.HIGHEST)
    wsq, gsq = lax.psum((wsq_local, gsq_local), ("replica", "spatial"))
    wnorm = jnp.sqrt(wsq)
    gnorm = jnp.sqrt(gsq)
    skipped = lars_skip.astype(jnp.float32)
    ratio = 0.02 * wnorm / (gnorm + 0.001 * wnorm + 1e-06)
    trust = skipped + (1.0 - skipped) * ratio
    decay = (1.0 - skipped) * 0.001
    trust_pos = jnp.dot(trust, onehot, precision=lax.Precision.HIGHEST)
    decay_pos = jnp.dot(decay, onehot, precision=lax.Precision.HIGHEST)
    new_velocity = 0.9 * velocity + 8.0 * trust_pos * (grad + decay_pos * master)
    new_master = master - new_velocity
    new_weights = lax.all_gather(
        new_master.astype(jnp.bfloat16), ("replica", "spatial"), axis=0, tiled=True
    )
    return (new_weights, new_master, new_velocity)


def solution(mesh):
    return jax.shard_map(
        shards,
        mesh=mesh,
        in_specs=(
            P("replica", "spatial", None),
            P(("replica", "spatial")),
            P(("replica", "spatial")),
            P(),
            P(),
            P(),
        ),
        out_specs=(P(), P(("replica", "spatial")), P(("replica", "spatial"))),
        check_vma=False,
    )
```

profile of v0, /device:TPU:0, one launch (start us, length us, event | category | flops | bytes accessed | tf_op | source)
XLA Modules:
  0.0 341.0 jit_solution(4959349934665128111)
XLA Ops:
  7.2 37.8 %reduce.1 = bf16[852992]{0:T(1024)(128)(2,1)} reduce(bf16[1,1,852992]{2,1,0:T(2,128)(2,1)} %param.6, bf16[]{:T(256)} %constant.38), dimensions={0,1}, to_apply=%param.6.reduce_sub_computation | reduce | bytes 3411970 | tf_op args[0]
  44.9 3.0 all_to_all.8
  47.9 0.5 broadcast.54
  48.4 13.3 %reduce.8 = bf16[16,53312]{1,0:T(8,128)(2,1)} reduce(bf16[16,1,53312]{2,1,0:T(2,128)(2,1)S(1)} %all_to_all.8, bf16[]{:T(256)} %broadcast.54), dimensions={1}, to_apply=%all_to_all.8.reduce_sub_computation | reduce | bytes 3411970 | tf_op jit(solution)/shard_map/all_to_all | solution.py:16
  61.8 3.2 reshape.38
  65.0 0.0 copy-start.1
  65.0 0.0 copy-start.4
  65.0 0.0 copy-start.6
  65.0 0.0 copy-start.7
  65.0 7.6 %all-to-all-start = ((bf16[16,2,26656]{2,1,0:T(2,128)(2,1)}), bf16[16,2,26656]{2,1,0:T(2,128)(2,1)}, u32[]{:S(2)}, u32[]{:S(2)}) async-start(bf16[16,2,26656]{2,1,0:T(2,128)(2,1)} %reshape.38), calls=%async_computation | async-start | bytes 3424256 | tf_op jit(solution)/shard_map/all_to_all | solution.py:16
  72.5 0.0 all-reduce.8.cloned.1.call-start
  72.6 0.0 copy-done.1
  72.6 0.7 reshape.25
  73.4 0.0 copy-done.4
  73.4 0.0 copy-done.6
  73.4 0.0 copy-done.7
  73.4 0.7 dynamic-slice
  74.1 0.7 iota_add_fusion
  74.7 32.2 %all-to-all-done = bf16[16,2,26656]{2,1,0:T(2,128)(2,1)} async-done(((bf16[16,2,26656]{2,1,0:T(2,128)(2,1)}), bf16[16,2,26656]{2,1,0:T(2,128)(2,1)}, u32[]{:S(2)}, u32[]{:S(2)}) %all-to-all-start) | async-done | bytes 1706016 | tf_op jit(solution)/shard_map/all_to_all | solution.py:16
  106.9 10.5 %reshape.39 = bf16[16,1,53312]{2,1,0:T(2,128)(2,1)S(1)} reshape(bf16[16,2,26656]{2,1,0:T(2,128)(2,1)} %all-to-all-done) | data formatting | bytes 3411968
  117.4 0.0 copy-start.5
  117.4 5.2 %convert_reduce_fusion = f32[53312]{0:T(1024)} fusion(bf16[16,1,53312]{2,1,0:T(2,128)(2,1)S(1)} %reshape.39), kind=kLoop, calls=%fused_computation | loop fusion | flops 1652672 | bytes 1919232 | tf_op jit(solution)/shard_map/reduce_sum | solution.py:23
  122.6 0.0 copy-start.3
  122.6 1.8 reshape.22
  124.5 0.0 all-reduce.8.cloned.1.call-update
  124.5 0.0 all-reduce.6.cloned.1.call-start
  124.5 0.0 copy-done.5
  124.5 1.7 convolution_reduce_fusion
  126.2 0.0 copy-start.2
  126.3 2.1 convolution_bitcast_fusion.1
  128.3 24.0 %all-reduce.8.cloned.1.call-done = f32[2,26656]{1,0:T(2,128)} async-done(((f32[2,26656]{1,0:T(2,128)}), f32[2,26656]{1,0:T(2,128)}) %all-reduce.8.cloned.1.call-update) | async-done | bytes 213264
  152.3 2.0 fusion
  154.3 0.1 reshape.27
  154.4 0.0 copy-done.3
  154.4 1.1 convolution_bitcast_fusion
  155.5 39.4 %all-reduce.2 = (f32[6]{0:T(128)S(1)}, f32[6]{0:T(128)S(1)}) all-reduce(f32[6]{0:T(128)S(1)} %convolution_bitcast_fusion, f32[6]{0:T(128)S(1)} %convolution_bitcast_fusion.1), channel_id=1, replica_groups=mesh['replica'=16,'spatial'=2] {'replica','spatial'}, use_global_device_ids=true, to_apply=%region_3.0 | all-reduce | flops 12 | bytes 96 | tf_op jit(solution)/shard_map/psum | solution.py:30
  194.9 0.8 convolution_reduce_fusion.1
  195.8 0.0 copy-done.2
  195.8 0.7 fusion.22
  196.5 0.1 broadcast.25
  196.6 0.6 dynamic-update-slice
  197.2 0.0 copy-start
  197.2 1.2 copy-done
  198.4 0.0 all-reduce.6.cloned.1.call-update
  198.4 133.0 %all-reduce.6.cloned.1.call-done = bf16[852992]{0:T(1024)(128)(2,1)} async-done(((bf16[852992]{0:T(1024)(128)(2,1)}), bf16[852992]{0:T(1024)(128)(2,1)}) %all-reduce.6.cloned.1.call-update) | async-done | bytes 1706000
  331.5 2.7 copy.13
  (3 shorter events, 0.0 us)
Async XLA Ops:
  65.0 7.7 %copy-start.1 = (f32[26656]{0:T(1024)S(1)}, f32[26656]{0:T(1024)}, u32[]{:S(2)}) copy-start(f32[26656]{0:T(1024)} %param.7) | copy-start | bytes 319876
  65.0 8.4 %copy-start.4 = (s32[6]{0:T(128)S(1)}, s32[6]{0:T(128)}, u32[]{:S(2)}) copy-start(s32[6]{0:T(128)} %param.10) | copy-start | bytes 76
  65.0 8.4 %copy-start.6 = (s32[6]{0:T(128)S(1)}, s32[6]{0:T(128)}, u32[]{:S(2)}) copy-start(s32[6]{0:T(128)} %param.9) | copy-start | bytes 76
  65.0 8.4 %copy-start.7 = (u32[32]{0:T(128)S(1)}, u32[32]{0:T(128)}, u32[]{:S(2)}) copy-start(u32[32]{0:T(128)} %constant.36) | copy-start | bytes 388
  65.0 41.9 %all-to-all-start = ((bf16[16,2,26656]{2,1,0:T(2,128)(2,1)}), bf16[16,2,26656]{2,1,0:T(2,128)(2,1)}, u32[]{:S(2)}, u32[]{:S(2)}) async-start(bf16[16,2,26656]{2,1,0:T(2,128)(2,1)} %reshape.38), calls=%async_computation | async-start | bytes 3424256 | tf_op jit(solution)/shard_map/all_to_all | solution.py:16
  72.5 79.8 %all-reduce.8.cloned.1.call-start = ((), (), s32[]{:S(2)}) async-start(), calls=%async_computation.2 | async-start | bytes 428032
  117.4 7.1 %copy-start.5 = (s32[6]{0:T(128)S(1)}, s32[6]{0:T(128)}, u32[]{:S(2)}) copy-start(s32[6]{0:T(128)} %param.11) | copy-start | bytes 76
  122.6 31.8 %copy-start.3 = (s32[26656]{0:T(1024)S(1)}, s32[26656]{0:T(1024)}, u32[]{:S(2)}) copy-start(s32[26656]{0:T(1024)} %iota_add_fusion) | copy-start | bytes 319876
  124.5 207.0 %all-reduce.6.cloned.1.call-start = ((), (), s32[]{:S(2)}) async-start(), calls=%async_computation.1 | async-start | bytes 3411968
  126.2 69.5 %copy-start.2 = (f32[26656]{0:T(1024)S(1)}, f32[26656]{0:T(1024)}, u32[]{:S(2)}) copy-start(f32[26656]{0:T(1024)} %param.8) | copy-start | bytes 319876
  197.2 1.2 copy-start
Sparse Core Ops, SparseCore 0:
  124.6 27.6 all-reduce.7
  198.6 132.8 all-reduce.5
where the time goes:
time: 342 us; the launch traced here: 341 us
  waiting for transfers between devices  189 us (55%)
  other arithmetic  59.7 us (17%)
  blocking collectives  39.4 us (12%)
  local copies, waits for them, and re-layouts  25.2 us (7%)
  between operations  14.2 us (4%)
  starting transfers between devices  7.66 us (2%)
  matrix products  5.68 us (2%)
    unnamed x4, waiting for transfers between devices  157 us
    psum x1, blocking collectives, shards(): wsq, gsq = lax.psum((wsq_local, gsq_local), ('replica', 'spatial'))  39.4 us
    unnamed x1, other arithmetic  37.8 us
    all_to_all x1, waiting for transfers between devices, shards(): lax.all_to_all(grads[0, 0].reshape(n_rep, n_spa * shard), 'replica', spli...  32.2 us
    unnamed x22, local copies, waits for them, and re-layouts  19.1 us
    all_to_all x1, other arithmetic, shards(): lax.all_to_all(grads[0, 0].reshape(n_rep, n_spa * shard), 'replica', spli...  13.3 us
    all_to_all x1, starting transfers between devices, shards(): lax.all_to_all(grads[0, 0].reshape(n_rep, n_spa * shard), 'replica', spli...  7.57 us
  transfers between devices with their start and end apart: 3, of which 3 were waited for; matrix products, arithmetic and copies ran while one was open for 2% of the time, Pallas kernels for 0%

commit v1 on v0

--- a/solution.py
+++ b/solution.py
@@ -2,6 +2,11 @@
 import jax.numpy as jnp
 from jax import lax
 from jax.sharding import PartitionSpec as P
+
+
+def assign_runs_all(my_tile, bus_axis, peer_axis):
+    high = jax.lax.psum(my_tile, bus_axis)
+    return jax.lax.psum(high, peer_axis)
 
 
 def shards(grads, master, velocity, layer_offsets, layer_sizes, lars_skip):
@@ -27,7 +32,7 @@
     grad = summed.reshape(shard) / (n_rep * n_spa)
     gsq_local = jnp.dot(onehot, grad * grad, precision=lax.Precision.HIGHEST)
     wsq_local = jnp.dot(onehot, master * master, precision=lax.Precision.HIGHEST)
-    wsq, gsq = lax.psum((wsq_local, gsq_local), ("replica", "spatial"))
+    wsq, gsq = assign_runs_all((wsq_local, gsq_local), "spatial", "replica")
     wnorm = jnp.sqrt(wsq)
     gnorm = jnp.sqrt(gsq)
     skipped = lars_skip.astype(jnp.float32)

time: 342 us -> 335 us (0.980)
  waiting for transfers between devices: 189 us -> 185 us
    unnamed x4, waiting for transfers between devices: 157 us -> 153 us
    psum x1 -> x2, blocking collectives: 39.4 us -> 36.6 us  [the longest x1 31.7 us: assign_runs_all(): return jax.lax.psum(high, peer_axis)]
where the time goes in v1:
time: 335 us; the launch traced here: 334 us
  waiting for transfers between devices  185 us (55%)
  other arithmetic  59.7 us (18%)
  blocking collectives  36.6 us (11%)
  local copies, waits for them, and re-layouts  25.2 us (8%)
  between operations  14.2 us (4%)
  starting transfers between devices  7.66 us (2%)
  matrix products  5.68 us (2%)
    unnamed x4, waiting for transfers between devices  153 us
    unnamed x1, other arithmetic  37.8 us
    all_to_all x1, waiting for transfers between devices, shards(): lax.all_to_all(grads[0, 0].reshape(n_rep, n_spa * shard), 'replica', spli...  32.2 us
    psum x1, blocking collectives, assign_runs_all(): return jax.lax.psum(high, peer_axis)  31.7 us
    unnamed x22, local copies, waits for them, and re-layouts  19.1 us
    all_to_all x1, other arithmetic, shards(): lax.all_to_all(grads[0, 0].reshape(n_rep, n_spa * shard), 'replica', spli...  13.3 us
    all_to_all x1, starting transfers between devices, shards(): lax.all_to_all(grads[0, 0].reshape(n_rep, n_spa * shard), 'replica', spli...  7.57 us
  transfers between devices with their start and end apart: 3, of which 3 were waited for; matrix products, arithmetic and copies ran while one was open for 2% of the time, Pallas kernels for 0%

profile of v1, /device:TPU:0, one launch (start us, length us, event | category | flops | bytes accessed | tf_op | source)
XLA Modules:
  0.0 334.0 jit_solution(1149764006265285418)
XLA Ops:
  7.2 37.8 %reduce.1 = bf16[852992]{0:T(1024)(128)(2,1)} reduce(bf16[1,1,852992]{2,1,0:T(2,128)(2,1)} %param.6, bf16[]{:T(256)} %constant.38), dimensions={0,1}, to_apply=%param.6.reduce_sub_computation | reduce | bytes 3411970 | tf_op args[0]
  44.9 3.0 all_to_all.8
  47.9 0.5 broadcast.54
  48.4 13.3 %reduce.8 = bf16[16,53312]{1,0:T(8,128)(2,1)} reduce(bf16[16,1,53312]{2,1,0:T(2,128)(2,1)S(1)} %all_to_all.8, bf16[]{:T(256)} %broadcast.54), dimensions={1}, to_apply=%all_to_all.8.reduce_sub_computation | reduce | bytes 3411970 | tf_op jit(solution)/shard_map/all_to_all | solution.py:21
  61.8 3.2 reshape.38
  65.0 0.0 copy-start.1
  65.0 0.0 copy-start.4
  65.0 0.0 copy-start.6
  65.0 0.0 copy-start.7
  65.0 7.6 %all-to-all-start = ((bf16[16,2,26656]{2,1,0:T(2,128)(2,1)}), bf16[16,2,26656]{2,1,0:T(2,128)(2,1)}, u32[]{:S(2)}, u32[]{:S(2)}) async-start(bf16[16,2,26656]{2,1,0:T(2,128)(2,1)} %reshape.38), calls=%async_computation | async-start | bytes 3424256 | tf_op jit(solution)/shard_map/all_to_all | solution.py:21
  72.5 0.0 all-reduce.9.cloned.1.call-start
  72.6 0.0 copy-done.1
  72.6 0.7 reshape.25
  73.4 0.0 copy-done.4
  73.4 0.0 copy-done.6
  73.4 0.0 copy-done.7
  73.4 0.7 dynamic-slice
  74.1 0.7 iota_add_fusion
  74.7 32.2 %all-to-all-done = bf16[16,2,26656]{2,1,0:T(2,128)(2,1)} async-done(((bf16[16,2,26656]{2,1,0:T(2,128)(2,1)}), bf16[16,2,26656]{2,1,0:T(2,128)(2,1)}, u32[]{:S(2)}, u32[]{:S(2)}) %all-to-all-start) | async-done | bytes 1706016 | tf_op jit(solution)/shard_map/all_to_all | solution.py:21
  106.9 10.5 %reshape.39 = bf16[16,1,53312]{2,1,0:T(2,128)(2,1)S(1)} reshape(bf16[16,2,26656]{2,1,0:T(2,128)(2,1)} %all-to-all-done) | data formatting | bytes 3411968
  117.4 0.0 copy-start.5
  117.4 5.2 %convert_reduce_fusion = f32[53312]{0:T(1024)} fusion(bf16[16,1,53312]{2,1,0:T(2,128)(2,1)S(1)} %reshape.39), kind=kLoop, calls=%fused_computation | loop fusion | flops 1652672 | bytes 1919232 | tf_op jit(solution)/shard_map/reduce_sum | solution.py:28
  122.6 0.0 copy-start.3
  122.6 1.8 reshape.22
  124.5 0.0 all-reduce.9.cloned.1.call-update
  124.5 0.0 all-reduce.7.cloned.1.call-start
  124.5 0.0 copy-done.5
  124.5 1.7 convolution_reduce_fusion
  126.2 0.0 copy-start.2
  126.3 2.1 convolution_bitcast_fusion.1
  128.3 24.0 %all-reduce.9.cloned.1.call-done = f32[2,26656]{1,0:T(2,128)} async-done(((f32[2,26656]{1,0:T(2,128)}), f32[2,26656]{1,0:T(2,128)}) %all-reduce.9.cloned.1.call-update) | async-done | bytes 213264
  152.3 2.0 fusion
  154.3 0.1 reshape.27
  154.4 0.0 copy-done.3
  154.4 1.1 convolution_bitcast_fusion
  155.5 4.9 %all-reduce.3 = (f32[6]{0:T(128)S(1)}, f32[6]{0:T(128)S(1)}) all-reduce(f32[6]{0:T(128)S(1)} %convolution_bitcast_fusion, f32[6]{0:T(128)S(1)} %convolution_bitcast_fusion.1), channel_id=1, replica_groups=mesh['replica'=16,'spatial'=2] {'spatial'}, use_global_device_ids=true, to_apply=%region_4.0 | all-reduce | flops 12 | bytes 96 | tf_op jit(solution)/shard_map/psum | solution.py:8
  160.4 31.7 %all-reduce.2 = (f32[6]{0:T(128)S(1)}, f32[6]{0:T(128)S(1)}) all-reduce(f32[6]{0:T(128)S(1)} %get-tuple-element.5, f32[6]{0:T(128)S(1)} %get-tuple-element.6), channel_id=1, replica_groups=mesh['replica'=16,'spatial'=2] {'replica'}, use_global_device_ids=true, to_apply=%region_5.0 | all-reduce | flops 12 | bytes 96 | tf_op jit(solution)/shard_map/psum | solution.py:9
  192.1 0.8 convolution_reduce_fusion.1
  192.9 0.0 copy-done.2
  192.9 0.7 fusion.22
  193.7 0.1 broadcast.25
  193.8 0.6 dynamic-update-slice
  194.4 0.0 copy-start
  194.4 1.2 copy-done
  195.6 0.0 all-reduce.7.cloned.1.call-update
  195.6 128.8 %all-reduce.7.cloned.1.call-done = bf16[852992]{0:T(1024)(128)(2,1)} async-done(((bf16[852992]{0:T(1024)(128)(2,1)}), bf16[852992]{0:T(1024)(128)(2,1)}) %all-reduce.7.cloned.1.call-update) | async-done | bytes 1706000
  324.4 2.7 copy.13
  (3 shorter events, 0.0 us)
Async XLA Ops:
  65.0 7.7 %copy-start.1 = (f32[26656]{0:T(1024)S(1)}, f32[26656]{0:T(1024)}, u32[]{:S(2)}) copy-start(f32[26656]{0:T(1024)} %param.7) | copy-start | bytes 319876
  65.0 8.4 %copy-start.4 = (s32[6]{0:T(128)S(1)}, s32[6]{0:T(128)}, u32[]{:S(2)}) copy-start(s32[6]{0:T(128)} %param.10) | copy-start | bytes 76
  65.0 8.4 %copy-start.6 = (s32[6]{0:T(128)S(1)}, s32[6]{0:T(128)}, u32[]{:S(2)}) copy-start(s32[6]{0:T(128)} %param.9) | copy-start | bytes 76
  65.0 8.4 %copy-start.7 = (u32[32]{0:T(128)S(1)}, u32[32]{0:T(128)}, u32[]{:S(2)}) copy-start(u32[32]{0:T(128)} %constant.36) | copy-start | bytes 388
  65.0 41.9 %all-to-all-start = ((bf16[16,2,26656]{2,1,0:T(2,128)(2,1)}), bf16[16,2,26656]{2,1,0:T(2,128)(2,1)}, u32[]{:S(2)}, u32[]{:S(2)}) async-start(bf16[16,2,26656]{2,1,0:T(2,128)(2,1)} %reshape.38), calls=%async_computation | async-start | bytes 3424256 | tf_op jit(solution)/shard_map/all_to_all | solution.py:21
  72.5 79.8 %all-reduce.9.cloned.1.call-start = ((), (), s32[]{:S(2)}) async-start(), calls=%async_computation.2 | async-start | bytes 428032
  117.4 7.1 %copy-start.5 = (s32[6]{0:T(128)S(1)}, s32[6]{0:T(128)}, u32[]{:S(2)}) copy-start(s32[6]{0:T(128)} %param.11) | copy-start | bytes 76
  122.6 31.8 %copy-start.3 = (s32[26656]{0:T(1024)S(1)}, s32[26656]{0:T(1024)}, u32[]{:S(2)}) copy-start(s32[26656]{0:T(1024)} %iota_add_fusion) | copy-start | bytes 319876
  124.5 199.9 %all-reduce.7.cloned.1.call-start = ((), (), s32[]{:S(2)}) async-start(), calls=%async_computation.1 | async-start | bytes 3411968
  126.2 66.7 %copy-start.2 = (f32[26656]{0:T(1024)S(1)}, f32[26656]{0:T(1024)}, u32[]{:S(2)}) copy-start(f32[26656]{0:T(1024)} %param.8) | copy-start | bytes 319876
  194.4 1.2 copy-start
Sparse Core Ops, SparseCore 0:
  124.6 27.6 all-reduce.8
  195.7 128.6 all-reduce.6
